TPU v7x, 32 devices: a whole 2x2x4 slice. The times are simulated.
32 devices in a mesh: row: 4 (over y, x), col: 8 (over z, core).
Axes of the slice: x: 2, y: 2, z: 4, core: 2. Of those that a mesh axis runs over, the one named last changes fastest.
Arguments:
- trial: bfloat16 [2, 512, 2048], P(None, 'row', 'col'), may hold values from -6 to 6
- val_energy: float32 [512], P('row'), may hold values from -1 to 0
- cond_energy: float32 [2048], P('col'), may hold values from 0.5 to 2
- val_orbitals: bfloat16 [512, 20480], P('col', 'row'), may hold values from -0.25 to 0.25
- cond_orbitals: bfloat16 [2048, 20480], P('row', 'col'), may hold values from -0.125 to 0.125
- screening: bfloat16 [20480, 20480], P('row', 'col'), may hold values from -0.29882812 to 0.29882812
Outputs:
- applied: float32 [2, 512, 2048], P(None, 'row', 'col')
All inputs are finite; a program needn't handle non-finite values.
Results may differ from a plain program's by a relative error of at most 0.0028.
Values may be sent and summed in bfloat16 or wider, within the bound.
No kernel may reach another device: no remote copies, remote signals or barrier semaphores. Data moves between devices by JAX's collectives and lax.ppermute only.
A program may use at most 128 MiB of HBM per device.

v0:
```python
import jax
import jax.numpy as jnp
from jax import lax
from jax.experimental import pallas as pl
from jax.experimental.pallas import tpu as pltpu
from jax.sharding import PartitionSpec as P


F32 = jnp.float32
BF16 = jnp.bfloat16
VMEM_LIMIT = 60 << 20


def whole(shape):
    return pl.BlockSpec(shape, lambda i: (0,) * len(shape))


def smem():
    return pl.BlockSpec(memory_space=pltpu.SMEM)


def params():
    return pltpu.CompilerParams(vmem_limit_bytes=VMEM_LIMIT)


def divisor(size, most):
    best = 128
    for d in range(128, most + 1, 128):
        if size % d == 0:
            best = d
    return best


def cost(flops, *arrays):
    moved = sum(x.size * x.dtype.itemsize for x in arrays)
    return pl.CostEstimate(flops=int(flops), bytes_accessed=int(moved), transcendentals=0)


def prepare(where, pieces, v):
    m = pieces[0].shape[1]
    mb = divisor(m, 1280)

    def body(where_ref, *refs):
        out = refs[-1]
        for i, piece in enumerate(refs[:-1]):
            rows = piece.shape[0]
            out[pl.ds(pl.multiple_of(where_ref[i], rows), rows), :] = piece[...]

    return pl.pallas_call(
        body,
        grid=(m // mb,),
        in_specs=[smem()] + [pl.BlockSpec((p.shape[0], mb), lambda i: (0, i)) for p in pieces],
        out_specs=pl.BlockSpec((v, mb), lambda i: (0, i)),
        out_shape=jax.ShapeDtypeStruct((v, m), BF16),
        compiler_params=params(),
        cost_estimate=cost(v * m * 800, *pieces),
        name="prepare",
    )(where, *pieces)


def encode(rows_at, core, mine, other, pieces):
    sides, v, lanes = mine.shape
    width, nj = pieces[0].shape
    n = len(pieces)

    def body(at_ref, core_ref, mine_ref, other_ref, *refs):
        hbm, (out, trial, cond, sems) = refs[:n], refs[n:]
        copies = [
            pltpu.make_async_copy(
                hbm[i], cond.at[pl.ds(pl.multiple_of(at_ref[i], width), width), :], sems.at[i]
            )
            for i in range(n)
        ]
        copies.append(pltpu.make_async_copy(mine_ref, trial.at[0], sems.at[n]))
        copies.append(pltpu.make_async_copy(other_ref, trial.at[1], sems.at[n + 1]))
        for copy in copies:
            copy.start()
        for copy in copies[:-1]:
            copy.wait()
        for b in range(2):
            if b == 1:
                copies[-1].wait()
            total = None
            for side in range(sides):
                part = jnp.dot(
                    trial[b, side], cond[side * lanes : (side + 1) * lanes, :], preferred_element_type=F32
                )
                total = part if total is None else total + part
            first = (core_ref[0] if b == 0 else 1 - core_ref[0]) * v
            out[pl.ds(pl.multiple_of(first, v), v), :] = total.astype(BF16)

    hbm = pl.BlockSpec(memory_space=pltpu.HBM)
    return pl.pallas_call(
        body,
        grid=(1,),
        in_specs=[smem(), smem()] + [hbm] * (n + 2),
        out_specs=whole((2 * v, nj)),
        out_shape=jax.ShapeDtypeStruct((2 * v, nj), BF16),
        scratch_shapes=[
            pltpu.VMEM((2, sides, v, lanes), BF16),
            pltpu.VMEM((sides * lanes, nj), BF16),
            pltpu.SemaphoreType.DMA((n + 2,)),
        ],
        compiler_params=params(),
        cost_estimate=cost(4 * v * sides * lanes * nj, mine, other, *pieces),
        name="encode",
    )(rows_at, core, mine, other, *pieces)


def screen(val, screening, enc, start):
    v, m = val.shape
    rows, nj = enc.shape
    mb = divisor(m, 1280)
    tile = divisor(nj, 512)

    def body(v_ref, s_ref, e_ref, out, total):
        i = pl.program_id(0)

        @pl.when(i == 0)
        def _():
            total[...] = jnp.zeros_like(total)

        for b in range(rows // v):
            for n in range(0, nj, tile):
                part = (slice(b * v, (b + 1) * v), slice(n, n + tile))
                moments = lax.dot_general(
                    v_ref[...], e_ref[part], (((0,), (0,)), ((), ())), preferred_element_type=F32
                )
                screened = (s_ref[:, n : n + tile].astype(F32) * moments).astype(BF16)
                total[part] += jnp.dot(v_ref[...], screened, preferred_element_type=F32)

        @pl.when(i == pl.num_programs(0) - 1)
        def _():
            out[...] = total[...].astype(BF16)

    return pl.pallas_call(
        body,
        grid=(m // mb,),
        in_specs=[
            pl.BlockSpec((v, mb), lambda i: (0, i)),
            pl.BlockSpec((mb, nj), lambda i: (i, start // nj)),
            whole(enc.shape),
        ],
        out_specs=whole((rows, nj)),
        out_shape=jax.ShapeDtypeStruct((rows, nj), BF16),
        scratch_shapes=[pltpu.VMEM((rows, nj), F32)],
        compiler_params=params(),
        cost_estimate=cost(4 * m * rows * nj, val, enc),
        name="screen",
    )(val, screening, enc)


def decode(rows_at, halves, pieces, b):
    v = halves[0].shape[0] // 2
    widths = [h.shape[1] for h in halves]
    width = pieces[0][0].shape[0]
    n, chunks = len(pieces[0]), len(halves)
    c = n * width

    def body(at_ref, *refs):
        h_refs = refs[:chunks]
        hbm = refs[chunks : chunks + n * chunks]
        outs = refs[chunks + n * chunks :][:2]
        held, sems = refs[-chunks - 1 : -1], refs[-1]
        copies = []
        for j in range(chunks):
            for i in range(n):
                at = pl.ds(pl.multiple_of(at_ref[i], width), width)
                copies.append(pltpu.make_async_copy(hbm[n * j + i], held[j].at[at, :], sems.at[i, j]))
                copies[-1].start()
        for side in range(2):
            total = None
            for j in range(chunks):
                if side == 0:
                    for copy in copies[n * j : n * (j + 1)]:
                        copy.wait()
                part = lax.dot_general(
                    held[j][side * (c // 2) : (side + 1) * (c // 2), :],
                    h_refs[j][...],
                    (((1,), (1,)), ((), ())),
                    preferred_element_type=F32,
                )
                total = part if total is None else total + part
            outs[side][...] = total.astype(outs[side].dtype)

    flat = [p for chunk in pieces for p in chunk]
    return pl.pallas_call(
        body,
        grid=(1,),
        in_specs=[smem()]
        + [pl.BlockSpec((v, nj), lambda i: (b, 0)) for nj in widths]
        + [pl.BlockSpec(memory_space=pltpu.HBM)] * len(flat),
        out_specs=[whole((c // 2, v))] * 2,
        out_shape=[jax.ShapeDtypeStruct((c // 2, v), t) for t in (F32, BF16)],
        scratch_shapes=[pltpu.VMEM((c, nj), BF16) for nj in widths] + [pltpu.SemaphoreType.DMA((n, chunks))],
        compiler_params=params(),
        cost_estimate=cost(2 * v * c * sum(widths), *flat),
        name="decode",
    )(rows_at, *halves, *flat)


def after(x, *first):
    return lax.optimization_barrier((x,) + first)[0]


def column_spans(n):
    unit = n // 5
    return ((4 * unit, unit), (0, 2 * unit), (2 * unit, 2 * unit))


def pipelined(rows_on, cols_on):
    chips = cols_on // 2

    def by_row(x, q):
        return lax.ppermute(x, "row", [(i, i ^ q) for i in range(rows_on)])

    def by_core(x):
        return lax.ppermute(x, "col", [(i, i ^ 1) for i in range(cols_on)])

    def by_chip(x, d):
        return lax.ppermute(x, "col", [(i, (i + 2 * d) % cols_on) for i in range(cols_on)])

    def near_rows(x):
        return [by_row(x, q) for q in range(1, 3 if rows_on == 4 else rows_on)]

    def over_rows(x, near):
        h = x.shape[0] // 2
        got = [(a[:h], a[h:]) for a in [x] + near]
        if rows_on == 4:
            got.append((by_row(got[2][0], 1), by_row(got[1][1], 2)))
        return got

    def local(trial, val_energy, cond_energy, val, cond, screening):
        _, v_own, c_own = trial.shape
        v, c = v_own * rows_on, c_own * cols_on
        k, n = val.shape[0], cond.shape[1]
        r = lax.axis_index("row")
        col = lax.axis_index("col")
        core, chip = col % 2, col // 2
        spans = column_spans(n)
        chunks = len(spans)

        def cut(x, at, size, axis):
            return lax.dynamic_slice_in_dim(x, at, size, axis)

        own = [cond[:, start : start + size] for start, size in spans]
        near, pieces = {}, []

        def ask(j, *first):
            if j < chunks:
                near[j] = near_rows(after(own[j], *first) if first else own[j])

        def ready(j):
            pieces.append([p for two in over_rows(own[j], near[j]) for p in two])

        partner = by_core(lax.dynamic_index_in_dim(trial, 1 - core, 0, False))
        ask(0)
        mine = lax.dynamic_index_in_dim(trial, core, 0, False)
        pair = jnp.where(core == 0, jnp.stack([mine, partner]), jnp.stack([partner, mine]))
        lane = jnp.zeros((2, v_own, c // 2), BF16)
        for d in range(chips):
            got = pair if d == 0 else by_chip(pair, d)
            lane = lax.dynamic_update_slice_in_dim(lane, got, (chip - d) % chips * c_own, 2)

        val_sent = after(val, lane)
        got_val = {d: by_chip(val_sent, d) for d in ((1, 3) if chips == 4 else range(1, chips))}
        placed = [(0, val)] + [(-d * 2 * k, x) for d, x in got_val.items()]
        if chips == 4:
            placed.append((-4 * k, by_chip(got_val[1][: k // 2], 1)))
            placed.append((-4 * k + k // 2, by_chip(got_val[3][k // 2 :], 3)))

        ready(0)
        near_trial = near_rows(lane)
        ask(1, *near_trial)
        full = jnp.zeros((2, v, c // 2), BF16)
        for q, two in enumerate(over_rows(lane, near_trial)):
            for side, got in enumerate(two):
                full = lax.dynamic_update_slice(full, got, (side, (r ^ q) * v_own, 0))
        full_other = by_core(full)

        at = [(side, c_own * (r ^ q)) for q in range(rows_on) for side in range(2)]
        core_of = jnp.stack([core])
        in_order = jnp.stack([side * (c // 2) + x for side, x in at])
        own_first = jnp.stack([jnp.where(side == core, 0, c // 2) + x for side, x in at])

        enc = encode(in_order, core_of, full, full_other, pieces[0])
        where, all_val = [], []
        for at, x in placed:
            where += [(2 * k * chip + at + k * core) % v, (2 * k * chip + at + k * (1 - core)) % v]
            all_val += [x, by_core(x)]
        ready(1)
        ask(2, *near[1])
        val_full = prepare(after(jnp.stack(where), enc), all_val, v)

        halves = []
        for j in range(chunks):
            if j == 0:
                enc = after(enc, *near[1])
            if j == 1:
                ready(2)
                enc = after(enc, *near[2])
            halves.append(screen(val_full, screening, enc, spans[j][0]))
            if j + 1 < chunks:
                enc = encode(after(in_order, halves[j]), core_of, full, full_other, pieces[j + 1])

        keep, give = decode(own_first, halves, pieces, 0)
        total = keep + by_core(give).astype(F32)
        sent = total.astype(BF16)
        first = cut(total, chip * c_own, c_own, 0)
        parts = [by_chip(cut(sent, (chip + d) % chips * c_own, c_own, 0), d) for d in range(1, chips)]

        keep, give = decode(after(own_first, give), halves, pieces, 1)
        total = keep + by_core(give).astype(F32)
        sent = total.astype(BF16)
        second = cut(total, r * v_own, v_own, 1)
        for q in range(1, rows_on):
            second += by_row(cut(sent, (r ^ q) * v_own, v_own, 1), q).astype(F32)
        for part in parts:
            first += part.astype(F32)

        sent = second.astype(BF16)
        second = cut(second, chip * c_own, c_own, 0)
        for d in range(1, chips):
            second += by_chip(cut(sent, (chip + d) % chips * c_own, c_own, 0), d).astype(F32)
        sent = first.astype(BF16)
        first = cut(first, r * v_own, v_own, 1)
        for q in range(1, rows_on):
            first += by_row(cut(sent, (r ^ q) * v_own, v_own, 1), q).astype(F32)
        gaps = cond_energy[None, None, :] - val_energy[None, :, None]
        return gaps * trial.astype(F32) + jnp.stack([first.T, second.T], axis=0)

    return local


def gathered(trial, val_energy, cond_energy, val_orbitals, cond_orbitals, screening):
    full_trial = lax.all_gather(trial, "col", axis=2, tiled=True)
    cond_full = lax.all_gather(cond_orbitals, "row", axis=0, tiled=True)
    val_full = lax.all_gather(val_orbitals, "col", axis=0, tiled=True)
    encoded = jnp.einsum("bvc,cn->bvn", full_trial, cond_full, preferred_element_type=F32).astype(BF16)
    scr_float = screening.astype(F32)
    pieces = []
    for b in range(trial.shape[0]):
        enc = lax.all_gather(encoded[b], "row", axis=0, tiled=True)
        moments = jnp.einsum("vm,vn->mn", val_full, enc, preferred_element_type=F32)
        screened = (scr_float * moments).astype(BF16)
        half = jnp.einsum("vm,mn->vn", val_full, screened, preferred_element_type=F32)
        half = lax.psum_scatter(half, "row", scatter_dimension=0, tiled=True).astype(BF16)
        part = jnp.einsum("vn,cn->vc", half, cond_full, preferred_element_type=F32)
        pieces.append(lax.psum_scatter(part, "col", scatter_dimension=1, tiled=True))
    gaps = cond_energy[None, None, :] - val_energy[None, :, None]
    return gaps * trial.astype(F32) + jnp.stack(pieces, axis=0)


def solution(mesh):
    rows_on, cols_on = mesh.shape["row"], mesh.shape["col"]
    placed = (
        P(None, "row", "col"),
        P("row"),
        P("col"),
        P("col", "row"),
        P("row", "col"),
        P("row", "col"),
    )

    def local(*args):
        trial = args[0]
        paired = cols_on == 2 * rows_on and trial.shape[0] == 2 and rows_on & (rows_on - 1) == 0
        aligned = trial.shape[2] % 128 == 0 and args[3].shape[0] % 32 == 0 and args[5].shape[1] % 640 == 0
        return (pipelined(rows_on, cols_on) if paired and aligned else gathered)(*args)

    return jax.shard_map(
        local, mesh=mesh, in_specs=placed, out_specs=P(None, "row", "col"), check_vma=False
    )
```

profile of v0, /device:TPU:0, one launch (start us, length us, event | category | flops | bytes accessed | tf_op | source)
XLA Modules:
  0.0 319.3 jit_solution(4928141381535929973)
XLA Ops:
  2.4 3.0 collective-permute-start.1
  11.9 5.1 %collective-permute-done.2 = bf16[2,128,256]{2,1,0:T(8,128)(2,1)S(1)} collective-permute-done((bf16[2,128,256]{2,1,0:T(8,128)(2,1)S(1)}, bf16[2,128,256]{2,1,0:T(8,128)(2,1)S(1)}, u32[]{:S(2)}, u32[]{:S(2)}) %collective-permute-start.2) | collective-permute-done | bytes 131104 | tf_op jit(solution)/shard_map/ppermute | solution.py:221
  26.1 5.9 %collective-permute-done.4 = bf16[2,128,1024]{2,1,0:T(8,128)(2,1)} collective-permute-done((bf16[2,128,1024]{2,1,0:T(8,128)(2,1)S(1)}, bf16[2,128,1024]{2,1,0:T(8,128)(2,1)}, u32[]{:S(2)}, u32[]{:S(2)}) %collective-permute-start.4) | collective-permute-done | bytes 524320 | tf_op jit(solution)/shard_map/ppermute | solution.py:215
  35.3 10.3 %collective-permute-done.5 = bf16[2,128,1024]{2,1,0:T(8,128)(2,1)S(1)} collective-permute-done((bf16[2,128,1024]{2,1,0:T(8,128)(2,1)S(1)}, bf16[2,128,1024]{2,1,0:T(8,128)(2,1)S(1)}, u32[]{:S(2)}, u32[]{:S(2)}) %collective-permute-start.5) | collective-permute-done | bytes 524320 | tf_op jit(solution)/shard_map/ppermute | solution.py:215
  51.2 4.4 %collective-permute-done.6 = bf16[1,128,1024]{2,1,0:T(8,128)(2,1)S(1)} collective-permute-done((bf16[1,128,1024]{2,1,0:T(8,128)(2,1)S(1)}, bf16[1,128,1024]{2,1,0:T(8,128)(2,1)S(1)}, u32[]{:S(2)}, u32[]{:S(2)}) %collective-permute-start.6) | collective-permute-done | bytes 262176 | tf_op jit(solution)/shard_map/ppermute | solution.py:215
  58.5 19.7 %collective-permute-done.7 = bf16[1,128,1024]{2,1,0:T(8,128)(2,1)S(1)} collective-permute-done((bf16[1,128,1024]{2,1,0:T(8,128)(2,1)S(1)}, bf16[1,128,1024]{2,1,0:T(8,128)(2,1)S(1)}, u32[]{:S(2)}, u32[]{:S(2)}) %collective-permute-start.7) | collective-permute-done | bytes 262176 | tf_op jit(solution)/shard_map/ppermute | solution.py:215
  79.0 3.5 %collective-permute-start.14 = (bf16[64,5120]{1,0:T(8,128)(2,1)S(1)}, bf16[64,5120]{1,0:T(8,128)(2,1)S(1)}, u32[]{:S(2)}, u32[]{:S(2)}) collective-permute-start(bf16[64,5120]{1,0:T(8,128)(2,1)S(1)} %copy-done.7), channel_id=1, source_target_pairs={{0,2},{1,3},{2,4},{3,5},{4,6},{5,7},{6,0},{7,1},{8,10},{9,11},{10,... | collective-permute-start | bytes 1966088 | tf_op jit(solution)/shard_map/ppermute | solution.py:221
  89.7 8.8 %collective-permute-done.14.refs_2_ = bf16[64,5120]{1,0:T(8,128)(2,1)S(1)} collective-permute-done((bf16[64,5120]{1,0:T(8,128)(2,1)S(1)}, bf16[64,5120]{1,0:T(8,128)(2,1)S(1)}, u32[]{:S(2)}, u32[]{:S(2)}) %collective-permute-start.14) | collective-permute-done | bytes 655392 | tf_op jit(solution)/shard_map/ppermute | solution.py:221
  100.0 12.2 %collective-permute-done.16.refs_4_ = bf16[64,5120]{1,0:T(8,128)(2,1)} collective-permute-done((bf16[64,5120]{1,0:T(8,128)(2,1)S(1)}, bf16[64,5120]{1,0:T(8,128)(2,1)}, u32[]{:S(2)}, u32[]{:S(2)}) %collective-permute-start.16) | collective-permute-done | bytes 655392 | tf_op jit(solution)/shard_map/ppermute | solution.py:221
  119.5 3.3 %collective-permute-start.20 = (bf16[32,5120]{1,0:T(8,128)(2,1)S(1)}, bf16[32,5120]{1,0:T(8,128)(2,1)}, u32[]{:S(2)}, u32[]{:S(2)}) collective-permute-start(bf16[32,5120]{1,0:T(8,128)(2,1)S(1)} %slice.133), channel_id=1, source_target_pairs={{0,6},{1,7},{2,0},{3,1},{4,2},{5,3},{6,4},{7,5},{8,14},{9,15},{10,... | collective-permute-start | bytes 983048 | tf_op jit(solution)/shard_map/ppermute | solution.py:221
  124.7 6.7 %collective-permute-done.18.refs_6_ = bf16[32,5120]{1,0:T(8,128)(2,1)} collective-permute-done((bf16[32,5120]{1,0:T(8,128)(2,1)S(1)}, bf16[32,5120]{1,0:T(8,128)(2,1)}, u32[]{:S(2)}, u32[]{:S(2)}) %collective-permute-start.18) | collective-permute-done | bytes 327712 | tf_op jit(solution)/shard_map/ppermute | solution.py:221
  131.4 4.3 %collective-permute-done.20.refs_8_ = bf16[32,5120]{1,0:T(8,128)(2,1)} collective-permute-done((bf16[32,5120]{1,0:T(8,128)(2,1)S(1)}, bf16[32,5120]{1,0:T(8,128)(2,1)}, u32[]{:S(2)}, u32[]{:S(2)}) %collective-permute-start.20) | collective-permute-done | bytes 327712 | tf_op jit(solution)/shard_map/ppermute | solution.py:221
  141.3 6.5 %encode.3.e_ref = bf16[1024,512]{1,0:T(8,128)(2,1)} custom-call(s32[8]{0:T(128)} %stack.139.at_ref, s32[1]{0:T(128)} %bitcast.26.core_ref, bf16[2,512,1024]{2,1,0:T(8,128)(2,1)} %constant_dynamic-update-slice_fusion.mine_ref, bf16[2,512,1024]{2,1,0:T(8,128)(2,1)} %collective-permute-done.8.other_ref, bf16[256,512]{1,0:T(8,128)(2,1)} %get-tuple-element.48.refs_0_.refs_3_, ...), custom_call_target="tpu_custom_call" | custom-call | flops 2147483648 | bytes 6291456 | tf_op jit(solution)/shard_map/encode/pallas_call | solution.py:93
  152.9 5.6 %prepare.1.v_ref = bf16[512,5120]{1,0:T(8,128)(2,1)} custom-call(s32[10]{0:T(128)} %stack.130.where_ref, bf16[64,5120]{1,0:T(8,128)(2,1)} %refs_0_.1, bf16[64,5120]{1,0:T(8,128)(2,1)} %copy-done.9, bf16[64,5120]{1,0:T(8,128)(2,1)} %copy-done.2, bf16[64,5120]{1,0:T(8,128)(2,1)} %copy-done.10, bf16[64,5120]{1,0:T(8,128)(2,1)} %collective-permute-done.16.refs_4_, ...), custom_call_target="tpu_custom_call" | custom-call | flops 2097152000 | bytes 5242880 | tf_op jit(solution)/shard_map/prepare/pallas_call | solution.py:49
  158.4 15.0 %screen.3.refs_0_ = bf16[1024,512]{1,0:T(8,128)(2,1)} custom-call(bf16[512,5120]{1,0:T(8,128)(2,1)} %prepare.1.v_ref, bf16[5120,2560]{1,0:T(8,128)(2,1)} %s_ref.5, bf16[1024,512]{1,0:T(8,128)(2,1)} %encode.3.e_ref), custom_call_target="tpu_custom_call" | custom-call | flops 10737418240 | bytes 6291456 | tf_op jit(solution)/shard_map/screen/pallas_call | solution.py:136
  174.2 9.6 %encode.4.e_ref = bf16[1024,1024]{1,0:T(8,128)(2,1)} custom-call(s32[8]{0:T(128)} %stack.139.at_ref, s32[1]{0:T(128)} %bitcast.26.core_ref, bf16[2,512,1024]{2,1,0:T(8,128)(2,1)} %constant_dynamic-update-slice_fusion.mine_ref, bf16[2,512,1024]{2,1,0:T(8,128)(2,1)} %collective-permute-done.8.other_ref, bf16[256,1024]{1,0:T(8,128)(2,1)} %get-tuple-element.43.refs_0_.refs_11_, ...), custom_call_target="tpu_custom_call" | custom-call | flops 4294967296 | bytes 8388608 | tf_op jit(solution)/shard_map/encode/pallas_call | solution.py:93
  183.9 27.3 %screen.4.refs_1_ = bf16[1024,1024]{1,0:T(8,128)(2,1)} custom-call(bf16[512,5120]{1,0:T(8,128)(2,1)} %prepare.1.v_ref, bf16[5120,2560]{1,0:T(8,128)(2,1)} %s_ref.5, bf16[1024,1024]{1,0:T(8,128)(2,1)} %encode.4.e_ref), custom_call_target="tpu_custom_call" | custom-call | flops 21474836480 | bytes 7340032 | tf_op jit(solution)/shard_map/screen/pallas_call | solution.py:136
  211.9 9.6 %encode.5.e_ref = bf16[1024,1024]{1,0:T(8,128)(2,1)} custom-call(s32[8]{0:T(128)} %stack.139.at_ref, s32[1]{0:T(128)} %bitcast.26.core_ref, bf16[2,512,1024]{2,1,0:T(8,128)(2,1)} %constant_dynamic-update-slice_fusion.mine_ref, bf16[2,512,1024]{2,1,0:T(8,128)(2,1)} %collective-permute-done.8.other_ref, bf16[256,1024]{1,0:T(8,128)(2,1)} %get-tuple-element.44.refs_0_.refs_19_, ...), custom_call_target="tpu_custom_call" | custom-call | flops 4294967296 | bytes 8388608 | tf_op jit(solution)/shard_map/encode/pallas_call | solution.py:93
  221.6 27.3 %screen.5.refs_2_ = bf16[1024,1024]{1,0:T(8,128)(2,1)} custom-call(bf16[512,5120]{1,0:T(8,128)(2,1)} %prepare.1.v_ref, bf16[5120,2560]{1,0:T(8,128)(2,1)} %s_ref.5, bf16[1024,1024]{1,0:T(8,128)(2,1)} %encode.5.e_ref), custom_call_target="tpu_custom_call" | custom-call | flops 21474836480 | bytes 7340032 | tf_op jit(solution)/shard_map/screen/pallas_call | solution.py:136
  248.9 11.4 %decode.2 = (f32[1024,512]{1,0:T(8,128)}, bf16[1024,512]{1,0:T(8,128)(2,1)}) custom-call(s32[8]{0:T(128)} %stack.119.at_ref, bf16[1024,512]{1,0:T(8,128)(2,1)} %screen.3.refs_0_, bf16[1024,1024]{1,0:T(8,128)(2,1)} %screen.4.refs_1_, bf16[1024,1024]{1,0:T(8,128)(2,1)} %screen.5.refs_2_, bf16[256,512]{1,0:T(8,128)(2,1)} %get-tuple-element.48.refs_0_.refs_3_, ...), custom_call_target="tpu_custom_call" | custom-call | flops 5368709120 | bytes 10485760 | tf_op jit(solution)/shard_map/decode/pallas_call | solution.py:187
  260.3 11.5 %decode.3 = (f32[1024,512]{1,0:T(8,128)}, bf16[1024,512]{1,0:T(8,128)(2,1)}) custom-call(s32[8]{0:T(128)} %stack.119.at_ref, bf16[1024,512]{1,0:T(8,128)(2,1)} %screen.3.refs_0_, bf16[1024,1024]{1,0:T(8,128)(2,1)} %screen.4.refs_1_, bf16[1024,1024]{1,0:T(8,128)(2,1)} %screen.5.refs_2_, bf16[256,512]{1,0:T(8,128)(2,1)} %get-tuple-element.48.refs_0_.refs_3_, ...), custom_call_target="tpu_custom_call" | custom-call | flops 5368709120 | bytes 10485760 | tf_op jit(solution)/shard_map/decode/pallas_call | solution.py:187
  289.0 3.0 collective-permute-done.39
  295.4 9.3 %collective-permute-start.41 = (bf16[256,128]{1,0:T(8,128)(2,1)S(1)}, bf16[256,128]{1,0:T(8,128)(2,1)S(1)}, u32[]{:S(2)}, u32[]{:S(2)}) collective-permute-start(bf16[256,128]{1,0:T(8,128)(2,1)S(1)} %get-tuple-element.74), channel_id=1, source_target_pairs={{0,2},{1,3},{2,4},{3,5},{4,6},{5,7},{6,0},{7,1},{8,10},{9,11},{10,... | collective-permute-start | bytes 196616 | tf_op jit(solution)/shard_map/ppermute | solution.py:221
  304.7 6.2 %collective-permute-done.32 = bf16[256,512]{1,0:T(8,128)(2,1)S(1)} collective-permute-done((bf16[256,512]{1,0:T(8,128)(2,1)S(1)}, bf16[256,512]{1,0:T(8,128)(2,1)S(1)}, u32[]{:S(2)}, u32[]{:S(2)}) %collective-permute-start.32) | collective-permute-done | bytes 262176 | tf_op jit(solution)/shard_map/ppermute | solution.py:221
  (157 shorter events, 89.6 us)
Async XLA Ops:
  20.5 58.5 %collective-permute-start.9 = (bf16[512,512]{1,0:T(8,128)(2,1)}, bf16[512,512]{1,0:T(8,128)(2,1)}, u32[]{:S(2)}, u32[]{:S(2)}) collective-permute-start(bf16[512,512]{1,0:T(8,128)(2,1)} %slice.101), channel_id=1, source_target_pairs={{0,8},{8,0},{16,24},{24,16},{1,9},{9,1},{17,25},{25,17},{2,10},{10... | collective-permute-start | bytes 1572872 | tf_op jit(solution)/shard_map/ppermute | solution.py:215
  21.0 61.5 %collective-permute-start.10 = (bf16[512,512]{1,0:T(8,128)(2,1)}, bf16[512,512]{1,0:T(8,128)(2,1)}, u32[]{:S(2)}, u32[]{:S(2)}) collective-permute-start(bf16[512,512]{1,0:T(8,128)(2,1)} %slice.101), channel_id=1, source_target_pairs={{0,16},{8,24},{16,0},{24,8},{1,17},{9,25},{17,1},{25,9},{2,18},{10... | collective-permute-start | bytes 1572872 | tf_op jit(solution)/shard_map/ppermute | solution.py:215
  22.5 23.1 %collective-permute-start.5 = (bf16[2,128,1024]{2,1,0:T(8,128)(2,1)S(1)}, bf16[2,128,1024]{2,1,0:T(8,128)(2,1)S(1)}, u32[]{:S(2)}, u32[]{:S(2)}) collective-permute-start(bf16[2,128,1024]{2,1,0:T(8,128)(2,1)S(1)} %constant_dynamic-update-slice_fusion.4), channel_id=1, source_target_pairs={{0,16},{8,24},{16,0},{24,8},{1,17},{9,25},{17,1},{25,9},{2,18},{10... | collective-permute-start | bytes 1572872 | tf_op jit(solution)/shard_map/ppermute | solution.py:215
  49.1 37.6 %collective-permute-start.22 = (bf16[512,1024]{1,0:T(8,128)(2,1)S(1)}, bf16[512,1024]{1,0:T(8,128)(2,1)S(1)}, u32[]{:S(2)}, u32[]{:S(2)}) collective-permute-start(bf16[512,1024]{1,0:T(8,128)(2,1)S(1)} %get-tuple-element.20), channel_id=1, source_target_pairs={{0,8},{8,0},{16,24},{24,16},{1,9},{9,1},{17,25},{25,17},{2,10},{10... | collective-permute-start | bytes 3145736 | tf_op jit(solution)/shard_map/ppermute | solution.py:215
  49.6 38.5 %collective-permute-start.23 = (bf16[512,1024]{1,0:T(8,128)(2,1)S(1)}, bf16[512,1024]{1,0:T(8,128)(2,1)S(1)}, u32[]{:S(2)}, u32[]{:S(2)}) collective-permute-start(bf16[512,1024]{1,0:T(8,128)(2,1)S(1)} %get-tuple-element.20), channel_id=1, source_target_pairs={{0,16},{8,24},{16,0},{24,8},{1,17},{9,25},{17,1},{25,9},{2,18},{10... | collective-permute-start | bytes 3145736 | tf_op jit(solution)/shard_map/ppermute | solution.py:215
  55.6 22.7 %collective-permute-start.7 = (bf16[1,128,1024]{2,1,0:T(8,128)(2,1)S(1)}, bf16[1,128,1024]{2,1,0:T(8,128)(2,1)S(1)}, u32[]{:S(2)}, u32[]{:S(2)}) collective-permute-start(bf16[1,128,1024]{2,1,0:T(8,128)(2,1)S(1)} %get-tuple-element.67), channel_id=1, source_target_pairs={{0,16},{8,24},{16,0},{24,8},{1,17},{9,25},{17,1},{25,9},{2,18},{10... | collective-permute-start | bytes 786440 | tf_op jit(solution)/shard_map/ppermute | solution.py:215
  79.0 59.6 %collective-permute-start.8 = (bf16[2,512,1024]{2,1,0:T(8,128)(2,1)}, bf16[2,512,1024]{2,1,0:T(8,128)(2,1)}, u32[]{:S(2)}, u32[]{:S(2)}) collective-permute-start(bf16[2,512,1024]{2,1,0:T(8,128)(2,1)} %constant_dynamic-update-slice_fusion.mine_ref), channel_id=1, source_target_pairs={{0,1},{1,0},{2,3},{3,2},{4,5},{5,4},{6,7},{7,6},{8,9},{9,8},{10,11... | collective-permute-start | bytes 6291464 | tf_op jit(solution)/shard_map/ppermute | solution.py:218
  79.0 19.5 %collective-permute-start.14 = (bf16[64,5120]{1,0:T(8,128)(2,1)S(1)}, bf16[64,5120]{1,0:T(8,128)(2,1)S(1)}, u32[]{:S(2)}, u32[]{:S(2)}) collective-permute-start(bf16[64,5120]{1,0:T(8,128)(2,1)S(1)} %copy-done.7), channel_id=1, source_target_pairs={{0,2},{1,3},{2,4},{3,5},{4,6},{5,7},{6,0},{7,1},{8,10},{9,11},{10,... | collective-permute-start | bytes 1966088 | tf_op jit(solution)/shard_map/ppermute | solution.py:221
  82.5 29.6 %collective-permute-start.16 = (bf16[64,5120]{1,0:T(8,128)(2,1)S(1)}, bf16[64,5120]{1,0:T(8,128)(2,1)}, u32[]{:S(2)}, u32[]{:S(2)}) collective-permute-start(bf16[64,5120]{1,0:T(8,128)(2,1)S(1)} %copy-done.7), channel_id=1, source_target_pairs={{0,6},{1,7},{2,0},{3,1},{4,2},{5,3},{6,4},{7,5},{8,14},{9,15},{10,... | collective-permute-start | bytes 1966088 | tf_op jit(solution)/shard_map/ppermute | solution.py:221
  86.6 32.2 %collective-permute-start.11 = (bf16[256,512]{1,0:T(8,128)(2,1)}, bf16[256,512]{1,0:T(8,128)(2,1)}, u32[]{:S(2)}, u32[]{:S(2)}) collective-permute-start(bf16[256,512]{1,0:T(8,128)(2,1)} %get-tuple-element.64.refs_4_.refs_7_), channel_id=1, source_target_pairs={{0,8},{8,0},{16,24},{24,16},{1,9},{9,1},{17,25},{25,17},{2,10},{10... | collective-permute-start | bytes 786440 | tf_op jit(solution)/shard_map/ppermute | solution.py:215
  88.1 31.4 %collective-permute-start.12 = (bf16[256,512]{1,0:T(8,128)(2,1)S(1)}, bf16[256,512]{1,0:T(8,128)(2,1)}, u32[]{:S(2)}, u32[]{:S(2)}) collective-permute-start(bf16[256,512]{1,0:T(8,128)(2,1)S(1)} %get-tuple-element.65.refs_3_.refs_6_), channel_id=1, source_target_pairs={{0,16},{8,24},{16,0},{24,8},{1,17},{9,25},{17,1},{25,9},{2,18},{10... | collective-permute-start | bytes 786440 | tf_op jit(solution)/shard_map/ppermute | solution.py:215
  98.5 37.2 %collective-permute-start.26 = (bf16[512,1024]{1,0:T(8,128)(2,1)}, bf16[512,1024]{1,0:T(8,128)(2,1)}, u32[]{:S(2)}, u32[]{:S(2)}) collective-permute-start(bf16[512,1024]{1,0:T(8,128)(2,1)} %get-tuple-element.23), channel_id=1, source_target_pairs={{0,8},{8,0},{16,24},{24,16},{1,9},{9,1},{17,25},{25,17},{2,10},{10... | collective-permute-start | bytes 3145736 | tf_op jit(solution)/shard_map/ppermute | solution.py:215
  112.1 26.4 %collective-permute-start.27 = (bf16[512,1024]{1,0:T(8,128)(2,1)}, bf16[512,1024]{1,0:T(8,128)(2,1)}, u32[]{:S(2)}, u32[]{:S(2)}) collective-permute-start(bf16[512,1024]{1,0:T(8,128)(2,1)} %get-tuple-element.23), channel_id=1, source_target_pairs={{0,16},{8,24},{16,0},{24,8},{1,17},{9,25},{17,1},{25,9},{2,18},{10... | collective-permute-start | bytes 3145736 | tf_op jit(solution)/shard_map/ppermute | solution.py:215
  131.4 16.4 %collective-permute-start.13 = (bf16[64,5120]{1,0:T(8,128)(2,1)S(1)}, bf16[64,5120]{1,0:T(8,128)(2,1)S(1)}, u32[]{:S(2)}, u32[]{:S(2)}) collective-permute-start(bf16[64,5120]{1,0:T(8,128)(2,1)S(1)} %copy-done.8), channel_id=1, source_target_pairs={{0,1},{1,0},{2,3},{3,2},{4,5},{5,4},{6,7},{7,6},{8,9},{9,8},{10,11... | collective-permute-start | bytes 1966088 | tf_op jit(solution)/shard_map/ppermute | solution.py:218
  135.7 16.3 %collective-permute-start.17 = (bf16[64,5120]{1,0:T(8,128)(2,1)}, bf16[64,5120]{1,0:T(8,128)(2,1)S(1)}, u32[]{:S(2)}, u32[]{:S(2)}) collective-permute-start(bf16[64,5120]{1,0:T(8,128)(2,1)} %collective-permute-done.16.refs_4_), channel_id=1, source_target_pairs={{0,1},{1,0},{2,3},{3,2},{4,5},{5,4},{6,7},{7,6},{8,9},{9,8},{10,11... | collective-permute-start | bytes 1966088 | tf_op jit(solution)/shard_map/ppermute | solution.py:218
  147.9 25.5 %collective-permute-start.24 = (bf16[256,1024]{1,0:T(8,128)(2,1)}, bf16[256,1024]{1,0:T(8,128)(2,1)S(1)}, u32[]{:S(2)}, u32[]{:S(2)}) collective-permute-start(bf16[256,1024]{1,0:T(8,128)(2,1)} %get-tuple-element.60.refs_4_.refs_15_), channel_id=1, source_target_pairs={{0,8},{8,0},{16,24},{24,16},{1,9},{9,1},{17,25},{25,17},{2,10},{10... | collective-permute-start | bytes 1572872 | tf_op jit(solution)/shard_map/ppermute | solution.py:215
  149.4 24.0 %collective-permute-start.25 = (bf16[256,1024]{1,0:T(8,128)(2,1)S(1)}, bf16[256,1024]{1,0:T(8,128)(2,1)}, u32[]{:S(2)}, u32[]{:S(2)}) collective-permute-start(bf16[256,1024]{1,0:T(8,128)(2,1)S(1)} %get-tuple-element.61.refs_3_.refs_14_), channel_id=1, source_target_pairs={{0,16},{8,24},{16,0},{24,8},{1,17},{9,25},{17,1},{25,9},{2,18},{10... | collective-permute-start | bytes 1572872 | tf_op jit(solution)/shard_map/ppermute | solution.py:215
  150.0 61.2 %collective-permute-start.28 = (bf16[256,1024]{1,0:T(8,128)(2,1)}, bf16[256,1024]{1,0:T(8,128)(2,1)}, u32[]{:S(2)}, u32[]{:S(2)}) collective-permute-start(bf16[256,1024]{1,0:T(8,128)(2,1)} %get-tuple-element.56.refs_4_.refs_23_), channel_id=1, source_target_pairs={{0,8},{8,0},{16,24},{24,16},{1,9},{9,1},{17,25},{25,17},{2,10},{10... | collective-permute-start | bytes 1572872 | tf_op jit(solution)/shard_map/ppermute | solution.py:215
  150.5 60.7 %collective-permute-start.29 = (bf16[256,1024]{1,0:T(8,128)(2,1)}, bf16[256,1024]{1,0:T(8,128)(2,1)S(1)}, u32[]{:S(2)}, u32[]{:S(2)}) collective-permute-start(bf16[256,1024]{1,0:T(8,128)(2,1)} %get-tuple-element.57.refs_3_.refs_22_), channel_id=1, source_target_pairs={{0,16},{8,24},{16,0},{24,8},{1,17},{9,25},{17,1},{25,9},{2,18},{10... | collective-permute-start | bytes 1572872 | tf_op jit(solution)/shard_map/ppermute | solution.py:215
  283.9 27.0 %collective-permute-start.32 = (bf16[256,512]{1,0:T(8,128)(2,1)S(1)}, bf16[256,512]{1,0:T(8,128)(2,1)S(1)}, u32[]{:S(2)}, u32[]{:S(2)}) collective-permute-start(bf16[256,512]{1,0:T(8,128)(2,1)S(1)} %get-tuple-element.51), channel_id=1, source_target_pairs={{0,4},{1,5},{2,6},{3,7},{4,0},{5,1},{6,2},{7,3},{8,12},{9,13},{10,... | collective-permute-start | bytes 786440 | tf_op jit(solution)/shard_map/ppermute | solution.py:221
  287.2 23.7 %collective-permute-start.31 = (bf16[256,512]{1,0:T(8,128)(2,1)S(1)}, bf16[256,512]{1,0:T(8,128)(2,1)S(1)}, u32[]{:S(2)}, u32[]{:S(2)}) collective-permute-start(bf16[256,512]{1,0:T(8,128)(2,1)S(1)} %get-tuple-element.49), channel_id=1, source_target_pairs={{0,2},{1,3},{2,4},{3,5},{4,6},{5,7},{6,0},{7,1},{8,10},{9,11},{10,... | collective-permute-start | bytes 786440 | tf_op jit(solution)/shard_map/ppermute | solution.py:221
  292.1 22.0 %collective-permute-start.43 = (bf16[256,128]{1,0:T(8,128)(2,1)S(1)}, bf16[256,128]{1,0:T(8,128)(2,1)S(1)}, u32[]{:S(2)}, u32[]{:S(2)}) collective-permute-start(bf16[256,128]{1,0:T(8,128)(2,1)S(1)} %get-tuple-element.75), channel_id=1, source_target_pairs={{0,6},{1,7},{2,0},{3,1},{4,2},{5,3},{6,4},{7,5},{8,14},{9,15},{10,... | collective-permute-start | bytes 196616 | tf_op jit(solution)/shard_map/ppermute | solution.py:221
  294.9 19.7 %collective-permute-start.42 = (bf16[256,128]{1,0:T(8,128)(2,1)S(1)}, bf16[256,128]{1,0:T(8,128)(2,1)S(1)}, u32[]{:S(2)}, u32[]{:S(2)}) collective-permute-start(bf16[256,128]{1,0:T(8,128)(2,1)S(1)} %get-tuple-element.76), channel_id=1, source_target_pairs={{0,4},{1,5},{2,6},{3,7},{4,0},{5,1},{6,2},{7,3},{8,12},{9,13},{10,... | collective-permute-start | bytes 196616 | tf_op jit(solution)/shard_map/ppermute | solution.py:221
  295.4 19.3 %collective-permute-start.41 = (bf16[256,128]{1,0:T(8,128)(2,1)S(1)}, bf16[256,128]{1,0:T(8,128)(2,1)S(1)}, u32[]{:S(2)}, u32[]{:S(2)}) collective-permute-start(bf16[256,128]{1,0:T(8,128)(2,1)S(1)} %get-tuple-element.74), channel_id=1, source_target_pairs={{0,2},{1,3},{2,4},{3,5},{4,6},{5,7},{6,0},{7,1},{8,10},{9,11},{10,... | collective-permute-start | bytes 196616 | tf_op jit(solution)/shard_map/ppermute | solution.py:221
  (40 other events, 456.6 us)
where the time goes:
time: 320 us; the launch traced here: 319 us
  Pallas kernels  124 us (39%)
  waiting for transfers between devices  98.6 us (31%)
  starting transfers between devices  60.9 us (19%)
  local copies, waits for them, and re-layouts  32.6 us (10%)
    pallas_call x3, Pallas kernels, screen(): pl.pallas_call(body, grid=(m // mb,), in_specs=[pl.BlockSpec((v, mb), lam...  69.6 us
    ppermute x22, waiting for transfers between devices, by_row(): return lax.ppermute(x, 'row', [(i, i ^ q) for i in range(rows_on)])  49.9 us
    ppermute x13, waiting for transfers between devices, by_chip(): lax.ppermute(x, 'col', [(i, (i + 2 * d) % cols_on) for i in range(cols_on)])  45.8 us
    ppermute x13, starting transfers between devices, by_chip(): lax.ppermute(x, 'col', [(i, (i + 2 * d) % cols_on) for i in range(cols_on)])  32.3 us
    ppermute x22, starting transfers between devices, by_row(): return lax.ppermute(x, 'row', [(i, i ^ q) for i in range(rows_on)])  26.4 us
    pallas_call x3, Pallas kernels, encode(): pl.pallas_call(body, grid=(1,), in_specs=[smem(), smem()] + [hbm] * (n +...  25.8 us
    pallas_call x2, Pallas kernels, decode(): pl.pallas_call(body, grid=(1,), in_specs=[smem()] + [pl.BlockSpec((v, nj)...  22.9 us
    slice x10, local copies, waits for them, and re-layouts, over_rows(): got = [(a[:h], a[h:]) for a in [x] + near]  15 us
  transfers between devices with their start and end apart: 44, of which 18 were waited for; matrix products, arithmetic and copies ran while one was open for 10% of the time, Pallas kernels for 20%

commit v1 on v0

--- a/solution.py
+++ b/solution.py
@@ -58,18 +58,21 @@
     )(where, *pieces)
 
 
-def encode(rows_at, core, mine, other, pieces):
+def encode(rows_at, core, mine, other, blocks, plan):
     sides, v, lanes = mine.shape
-    width, nj = pieces[0].shape
-    n = len(pieces)
+    nj = blocks[0].shape[1]
+    n = len(plan)
+    width = sides * lanes // n
 
     def body(at_ref, core_ref, mine_ref, other_ref, *refs):
-        hbm, (out, trial, cond, sems) = refs[:n], refs[n:]
+        hbm, (out, trial, cond, sems) = refs[: len(blocks)], refs[len(blocks) :]
         copies = [
             pltpu.make_async_copy(
-                hbm[i], cond.at[pl.ds(pl.multiple_of(at_ref[i], width), width), :], sems.at[i]
+                hbm[block].at[pl.ds(first, width), :],
+                cond.at[pl.ds(pl.multiple_of(at_ref[i], width), width), :],
+                sems.at[i],
             )
-            for i in range(n)
+            for i, (block, first) in enumerate(plan)
         ]
         copies.append(pltpu.make_async_copy(mine_ref, trial.at[0], sems.at[n]))
         copies.append(pltpu.make_async_copy(other_ref, trial.at[1], sems.at[n + 1]))
@@ -93,7 +96,7 @@
     return pl.pallas_call(
         body,
         grid=(1,),
-        in_specs=[smem(), smem()] + [hbm] * (n + 2),
+        in_specs=[smem(), smem()] + [hbm] * (len(blocks) + 2),
         out_specs=whole((2 * v, nj)),
         out_shape=jax.ShapeDtypeStruct((2 * v, nj), BF16),
         scratch_shapes=[
@@ -102,9 +105,9 @@
             pltpu.SemaphoreType.DMA((n + 2,)),
         ],
         compiler_params=params(),
-        cost_estimate=cost(4 * v * sides * lanes * nj, mine, other, *pieces),
+        cost_estimate=cost(4 * v * sides * lanes * nj, mine, other, *blocks),
         name="encode",
-    )(rows_at, core, mine, other, *pieces)
+    )(rows_at, core, mine, other, *blocks)
 
 
 def screen(val, screening, enc, start):
@@ -150,23 +153,24 @@
     )(val, screening, enc)
 
 
-def decode(rows_at, halves, pieces, b):
+def decode(rows_at, halves, blocks, plan, b):
     v = halves[0].shape[0] // 2
     widths = [h.shape[1] for h in halves]
-    width = pieces[0][0].shape[0]
-    n, chunks = len(pieces[0]), len(halves)
+    held_by, n, chunks = len(blocks[0]), len(plan), len(halves)
+    width = blocks[0][-1].shape[0] if plan[-1][1] == 0 else plan[-1][1]
     c = n * width
 
     def body(at_ref, *refs):
         h_refs = refs[:chunks]
-        hbm = refs[chunks : chunks + n * chunks]
-        outs = refs[chunks + n * chunks :][:2]
+        hbm = refs[chunks : chunks + held_by * chunks]
+        outs = refs[chunks + held_by * chunks :][:2]
         held, sems = refs[-chunks - 1 : -1], refs[-1]
         copies = []
         for j in range(chunks):
-            for i in range(n):
+            for i, (block, first) in enumerate(plan):
                 at = pl.ds(pl.multiple_of(at_ref[i], width), width)
-                copies.append(pltpu.make_async_copy(hbm[n * j + i], held[j].at[at, :], sems.at[i, j]))
+                piece = hbm[held_by * j + block].at[pl.ds(first, width), :]
+                copies.append(pltpu.make_async_copy(piece, held[j].at[at, :], sems.at[i, j]))
                 copies[-1].start()
         for side in range(2):
             total = None
@@ -183,7 +187,7 @@
                 total = part if total is None else total + part
             outs[side][...] = total.astype(outs[side].dtype)
 
-    flat = [p for chunk in pieces for p in chunk]
+    flat = [x for chunk in blocks for x in chunk]
     return pl.pallas_call(
         body,
         grid=(1,),
@@ -244,14 +248,21 @@
             return lax.dynamic_slice_in_dim(x, at, size, axis)
 
         own = [cond[:, start : start + size] for start, size in spans]
-        near, pieces = {}, []
+        near, blocks = {}, []
+        plan = [(q, side * c_own) for q in range(rows_on) for side in range(2)]
+        if rows_on == 4:
+            plan[-2:] = [(3, 0), (4, 0)]
 
         def ask(j, *first):
             if j < chunks:
                 near[j] = near_rows(after(own[j], *first) if first else own[j])
 
         def ready(j):
-            pieces.append([p for two in over_rows(own[j], near[j]) for p in two])
+            got = [own[j]] + near[j]
+            if rows_on == 4:
+                got.append(by_row(near[j][1][:c_own], 1))
+                got.append(by_row(near[j][0][c_own:], 2))
+            blocks.append(got)
 
         partner = by_core(lax.dynamic_index_in_dim(trial, 1 - core, 0, False))
         ask(0)
@@ -283,7 +294,7 @@
         in_order = jnp.stack([side * (c // 2) + x for side, x in at])
         own_first = jnp.stack([jnp.where(side == core, 0, c // 2) + x for side, x in at])
 
-        enc = encode(in_order, core_of, full, full_other, pieces[0])
+        enc = encode(in_order, core_of, full, full_other, blocks[0], plan)
         where, all_val = [], []
         for at, x in placed:
             where += [(2 * k * chip + at + k * core) % v, (2 * k * chip + at + k * (1 - core)) % v]
@@ -301,15 +312,15 @@
                 enc = after(enc, *near[2])
             halves.append(screen(val_full, screening, enc, spans[j][0]))
             if j + 1 < chunks:
-                enc = encode(after(in_order, halves[j]), core_of, full, full_other, pieces[j + 1])
-
-        keep, give = decode(own_first, halves, pieces, 0)
+                enc = encode(after(in_order, halves[j]), core_of, full, full_other, blocks[j + 1], plan)
+
+        keep, give = decode(own_first, halves, blocks, plan, 0)
         total = keep + by_core(give).astype(F32)
         sent = total.astype(BF16)
         first = cut(total, chip * c_own, c_own, 0)
         parts = [by_chip(cut(sent, (chip + d) % chips * c_own, c_own, 0), d) for d in range(1, chips)]
 
-        keep, give = decode(after(own_first, give), halves, pieces, 1)
+        keep, give = decode(after(own_first, give), halves, blocks, plan, 1)
         total = keep + by_core(give).astype(F32)
         sent = total.astype(BF16)
         second = cut(total, r * v_own, v_own, 1)

time: 320 us -> 338 us (1.056)
  waiting for transfers between devices: 98.6 us -> 123 us
  local copies, waits for them, and re-layouts: 32.6 us -> 22.4 us
    ppermute x22, waiting for transfers between devices: 49.9 us -> 100 us  [by_row(): return lax.ppermute(x, 'row', [(i, i ^ q) for i in range(rows_on)])]
    ppermute x13, waiting for transfers between devices: 45.8 us -> 20.3 us  [by_chip(): lax.ppermute(x, 'col', [(i, (i + 2 * d) % cols_on) for i in range(cols_on)])]
    slice x10 -> x2, local copies, waits for them, and re-layouts: 15 us -> 2.55 us  [over_rows(): got = [(a[:h], a[h:]) for a in [x] + near]]
    ppermute x13, starting transfers between devices: 32.3 us -> 37.5 us  [by_chip(): lax.ppermute(x, 'col', [(i, (i + 2 * d) % cols_on) for i in range(cols_on)])]
    dynamic_update_slice x6, local copies, waits for them, and re-layouts: 5.31 us -> 1.08 us  [local(): full = lax.dynamic_update_slice(full, got, (side, (r ^ q) * v_own, 0))]
    slice x0 -> x6, local copies, waits for them, and re-layouts: none -> 4.04 us  [the longest x3 2.09 us: ready(): got.append(by_row(near[j][1][:c_own], 1))]
  transfers between devices with their start and end apart: 44 -> 44, of which waited for: 18 -> 18; matrix products, arithmetic and copies ran while one was open for 10% -> 6% of each run, Pallas kernels for 20% -> 19%
where the time goes in v1:
time: 338 us
  Pallas kernels  124 us (37%)
  waiting for transfers between devices  123 us (36%)
  starting transfers between devices  64.2 us (19%)
  local copies, waits for them, and re-layouts  22.4 us (7%)
    ppermute x22, waiting for transfers between devices, by_row(): return lax.ppermute(x, 'row', [(i, i ^ q) for i in range(rows_on)])  100 us
    pallas_call x3, Pallas kernels, screen(): pl.pallas_call(body, grid=(m // mb,), in_specs=[pl.BlockSpec((v, mb), lam...  69.5 us
    ppermute x13, starting transfers between devices, by_chip(): lax.ppermute(x, 'col', [(i, (i + 2 * d) % cols_on) for i in range(cols_on)])  37.5 us
    pallas_call x3, Pallas kernels, encode(): pl.pallas_call(body, grid=(1,), in_specs=[smem(), smem()] + [hbm] * (len(...  25.9 us
    ppermute x22, starting transfers between devices, by_row(): return lax.ppermute(x, 'row', [(i, i ^ q) for i in range(rows_on)])  24.7 us
    pallas_call x2, Pallas kernels, decode(): pl.pallas_call(body, grid=(1,), in_specs=[smem()] + [pl.BlockSpec((v, nj)...  22.9 us
    ppermute x13, waiting for transfers between devices, by_chip(): lax.ppermute(x, 'col', [(i, (i + 2 * d) % cols_on) for i in range(cols_on)])  20.3 us
  transfers between devices with their start and end apart: 44, of which 18 were waited for; matrix products, arithmetic and copies ran while one was open for 6% of the time, Pallas kernels for 19%

profile of v1, /device:TPU:0, one launch (start us, length us, event | category | flops | bytes accessed | tf_op | source)
XLA Modules:
  0.0 337.5 jit_solution(13258386258695546752)
XLA Ops:
  11.9 5.1 %collective-permute-done.2 = bf16[2,128,256]{2,1,0:T(8,128)(2,1)S(1)} collective-permute-done((bf16[2,128,256]{2,1,0:T(8,128)(2,1)S(1)}, bf16[2,128,256]{2,1,0:T(8,128)(2,1)S(1)}, u32[]{:S(2)}, u32[]{:S(2)}) %collective-permute-start.2) | collective-permute-done | bytes 131104 | tf_op jit(solution)/shard_map/ppermute | solution.py:225
  23.4 7.4 %collective-permute-done.5 = bf16[2,128,1024]{2,1,0:T(8,128)(2,1)S(1)} collective-permute-done((bf16[2,128,1024]{2,1,0:T(8,128)(2,1)S(1)}, bf16[2,128,1024]{2,1,0:T(8,128)(2,1)S(1)}, u32[]{:S(2)}, u32[]{:S(2)}) %collective-permute-start.5) | collective-permute-done | bytes 524320 | tf_op jit(solution)/shard_map/ppermute | solution.py:219
  39.8 22.1 %collective-permute-done.6 = bf16[1,128,1024]{2,1,0:T(8,128)(2,1)S(1)} collective-permute-done((bf16[1,128,1024]{2,1,0:T(8,128)(2,1)}, bf16[1,128,1024]{2,1,0:T(8,128)(2,1)S(1)}, u32[]{:S(2)}, u32[]{:S(2)}) %collective-permute-start.6) | collective-permute-done | bytes 262176 | tf_op jit(solution)/shard_map/ppermute | solution.py:219
  61.9 5.0 %collective-permute-done.7 = bf16[1,128,1024]{2,1,0:T(8,128)(2,1)S(1)} collective-permute-done((bf16[1,128,1024]{2,1,0:T(8,128)(2,1)}, bf16[1,128,1024]{2,1,0:T(8,128)(2,1)S(1)}, u32[]{:S(2)}, u32[]{:S(2)}) %collective-permute-start.7) | collective-permute-done | bytes 262176 | tf_op jit(solution)/shard_map/ppermute | solution.py:219
  70.6 3.4 %collective-permute-start.14 = (bf16[64,5120]{1,0:T(8,128)(2,1)S(1)}, bf16[64,5120]{1,0:T(8,128)(2,1)S(1)}, u32[]{:S(2)}, u32[]{:S(2)}) collective-permute-start(bf16[64,5120]{1,0:T(8,128)(2,1)S(1)} %copy-done.3), channel_id=1, source_target_pairs={{0,2},{1,3},{2,4},{3,5},{4,6},{5,7},{6,0},{7,1},{8,10},{9,11},{10,... | collective-permute-start | bytes 1966088 | tf_op jit(solution)/shard_map/ppermute | solution.py:225
  74.6 7.9 %collective-permute-done.10.refs_2_.refs_5_ = bf16[512,512]{1,0:T(8,128)(2,1)S(1)} collective-permute-done((bf16[512,512]{1,0:T(8,128)(2,1)S(1)}, bf16[512,512]{1,0:T(8,128)(2,1)S(1)}, u32[]{:S(2)}, u32[]{:S(2)}) %collective-permute-start.10) | collective-permute-done | bytes 524320 | tf_op jit(solution)/shard_map/ppermute | solution.py:219
  82.5 3.1 collective-permute-start.16
  87.2 23.7 %collective-permute-done.11.refs_3_.refs_6_ = bf16[256,512]{1,0:T(8,128)(2,1)S(1)} collective-permute-done((bf16[256,512]{1,0:T(8,128)(2,1)S(1)}, bf16[256,512]{1,0:T(8,128)(2,1)S(1)}, u32[]{:S(2)}, u32[]{:S(2)}) %collective-permute-start.11) | collective-permute-done | bytes 262176 | tf_op jit(solution)/shard_map/ppermute | solution.py:219
  113.0 3.5 %collective-permute-start.18 = (bf16[32,5120]{1,0:T(8,128)(2,1)S(1)}, bf16[32,5120]{1,0:T(8,128)(2,1)}, u32[]{:S(2)}, u32[]{:S(2)}) collective-permute-start(bf16[32,5120]{1,0:T(8,128)(2,1)S(1)} %slice.76), channel_id=1, source_target_pairs={{0,2},{1,3},{2,4},{3,5},{4,6},{5,7},{6,0},{7,1},{8,10},{9,11},{10,... | collective-permute-start | bytes 983048 | tf_op jit(solution)/shard_map/ppermute | solution.py:225
  117.5 23.1 %collective-permute-done.12.refs_4_.refs_7_ = bf16[256,512]{1,0:T(8,128)(2,1)S(1)} collective-permute-done((bf16[256,512]{1,0:T(8,128)(2,1)S(1)}, bf16[256,512]{1,0:T(8,128)(2,1)S(1)}, u32[]{:S(2)}, u32[]{:S(2)}) %collective-permute-start.12) | collective-permute-done | bytes 262176 | tf_op jit(solution)/shard_map/ppermute | solution.py:219
  143.8 6.4 %collective-permute-done.20.refs_8_ = bf16[32,5120]{1,0:T(8,128)(2,1)} collective-permute-done((bf16[32,5120]{1,0:T(8,128)(2,1)S(1)}, bf16[32,5120]{1,0:T(8,128)(2,1)}, u32[]{:S(2)}, u32[]{:S(2)}) %collective-permute-start.20) | collective-permute-done | bytes 327712 | tf_op jit(solution)/shard_map/ppermute | solution.py:225
  159.4 6.6 %encode.3.e_ref = bf16[1024,512]{1,0:T(8,128)(2,1)} custom-call(s32[8]{0:T(128)} %stack.139.at_ref, s32[1]{0:T(128)} %bitcast.26.core_ref, bf16[2,512,1024]{2,1,0:T(8,128)(2,1)} %copy-done.1, bf16[2,512,1024]{2,1,0:T(8,128)(2,1)} %copy-done.17, bf16[512,512]{1,0:T(8,128)(2,1)} %copy-done.4, bf16[512,512]{1,0:T(8,128)(2,1)} %copy-done.14, ...), custom_call_target="tpu_custom_call" | custom-call | flops 2147483648 | bytes 6291456 | tf_op jit(solution)/shard_map/encode/pallas_call | solution.py:96
  170.1 5.6 %prepare.1.v_ref = bf16[512,5120]{1,0:T(8,128)(2,1)} custom-call(s32[10]{0:T(128)} %stack.130.where_ref, bf16[64,5120]{1,0:T(8,128)(2,1)} %refs_0_.1, bf16[64,5120]{1,0:T(8,128)(2,1)} %collective-permute-done.13.refs_1_, bf16[64,5120]{1,0:T(8,128)(2,1)} %copy-done.2, bf16[64,5120]{1,0:T(8,128)(2,1)} %collective-permute-done.15.refs_3_, ...), custom_call_target="tpu_custom_call" | custom-call | flops 2097152000 | bytes 5242880 | tf_op jit(solution)/shard_map/prepare/pallas_call | solution.py:49
  175.7 15.0 %screen.3.refs_0_ = bf16[1024,512]{1,0:T(8,128)(2,1)} custom-call(bf16[512,5120]{1,0:T(8,128)(2,1)} %prepare.1.v_ref, bf16[5120,2560]{1,0:T(8,128)(2,1)} %s_ref.5, bf16[1024,512]{1,0:T(8,128)(2,1)} %encode.3.e_ref), custom_call_target="tpu_custom_call" | custom-call | flops 10737418240 | bytes 6291456 | tf_op jit(solution)/shard_map/screen/pallas_call | solution.py:139
  192.4 9.6 %encode.4.e_ref = bf16[1024,1024]{1,0:T(8,128)(2,1)} custom-call(s32[8]{0:T(128)} %stack.139.at_ref, s32[1]{0:T(128)} %bitcast.26.core_ref, bf16[2,512,1024]{2,1,0:T(8,128)(2,1)} %copy-done.1, bf16[2,512,1024]{2,1,0:T(8,128)(2,1)} %copy-done.17, bf16[512,1024]{1,0:T(8,128)(2,1)} %get-tuple-element.20.refs_0_.refs_8_, ...), custom_call_target="tpu_custom_call" | custom-call | flops 4294967296 | bytes 8388608 | tf_op jit(solution)/shard_map/encode/pallas_call | solution.py:96
  202.0 27.2 %screen.4.refs_1_ = bf16[1024,1024]{1,0:T(8,128)(2,1)} custom-call(bf16[512,5120]{1,0:T(8,128)(2,1)} %prepare.1.v_ref, bf16[5120,2560]{1,0:T(8,128)(2,1)} %s_ref.5, bf16[1024,1024]{1,0:T(8,128)(2,1)} %encode.4.e_ref), custom_call_target="tpu_custom_call" | custom-call | flops 21474836480 | bytes 7340032 | tf_op jit(solution)/shard_map/screen/pallas_call | solution.py:139
  230.1 9.6 %encode.5.e_ref = bf16[1024,1024]{1,0:T(8,128)(2,1)} custom-call(s32[8]{0:T(128)} %stack.139.at_ref, s32[1]{0:T(128)} %bitcast.26.core_ref, bf16[2,512,1024]{2,1,0:T(8,128)(2,1)} %copy-done.1, bf16[2,512,1024]{2,1,0:T(8,128)(2,1)} %copy-done.17, bf16[512,1024]{1,0:T(8,128)(2,1)} %get-tuple-element.23.refs_0_.refs_13_, bf16[512,1024]{1,0:T(8,128)(2,1)} %copy-done.9, ...), custom_call_target="tpu_custom_call" | custom-call | flops 4294967296 | bytes 8388608 | tf_op jit(solution)/shard_map/encode/pallas_call | solution.py:96
  239.8 27.3 %screen.5.refs_2_ = bf16[1024,1024]{1,0:T(8,128)(2,1)} custom-call(bf16[512,5120]{1,0:T(8,128)(2,1)} %prepare.1.v_ref, bf16[5120,2560]{1,0:T(8,128)(2,1)} %s_ref.5, bf16[1024,1024]{1,0:T(8,128)(2,1)} %encode.5.e_ref), custom_call_target="tpu_custom_call" | custom-call | flops 21474836480 | bytes 7340032 | tf_op jit(solution)/shard_map/screen/pallas_call | solution.py:139
  267.1 11.4 %decode.2 = (f32[1024,512]{1,0:T(8,128)}, bf16[1024,512]{1,0:T(8,128)(2,1)}) custom-call(s32[8]{0:T(128)} %stack.119.at_ref, bf16[1024,512]{1,0:T(8,128)(2,1)} %screen.3.refs_0_, bf16[1024,1024]{1,0:T(8,128)(2,1)} %screen.4.refs_1_, bf16[1024,1024]{1,0:T(8,128)(2,1)} %screen.5.refs_2_, bf16[512,512]{1,0:T(8,128)(2,1)} %copy-done.4, ...), custom_call_target="tpu_custom_call" | custom-call | flops 5368709120 | bytes 10485760 | tf_op jit(solution)/shard_map/decode/pallas_call | solution.py:191
  278.5 11.5 %decode.3 = (f32[1024,512]{1,0:T(8,128)}, bf16[1024,512]{1,0:T(8,128)(2,1)}) custom-call(s32[8]{0:T(128)} %stack.119.at_ref, bf16[1024,512]{1,0:T(8,128)(2,1)} %screen.3.refs_0_, bf16[1024,1024]{1,0:T(8,128)(2,1)} %screen.4.refs_1_, bf16[1024,1024]{1,0:T(8,128)(2,1)} %screen.5.refs_2_, bf16[512,512]{1,0:T(8,128)(2,1)} %copy-done.4, ...), custom_call_target="tpu_custom_call" | custom-call | flops 5368709120 | bytes 10485760 | tf_op jit(solution)/shard_map/decode/pallas_call | solution.py:191
  299.3 3.3 collective-permute-start.33
  310.4 3.3 collective-permute-start.43
  313.6 9.2 %collective-permute-start.41 = (bf16[256,128]{1,0:T(8,128)(2,1)S(1)}, bf16[256,128]{1,0:T(8,128)(2,1)S(1)}, u32[]{:S(2)}, u32[]{:S(2)}) collective-permute-start(bf16[256,128]{1,0:T(8,128)(2,1)S(1)} %get-tuple-element.56), channel_id=1, source_target_pairs={{0,2},{1,3},{2,4},{3,5},{4,6},{5,7},{6,0},{7,1},{8,10},{9,11},{10,... | collective-permute-start | bytes 196616 | tf_op jit(solution)/shard_map/ppermute | solution.py:225
  322.9 6.3 %collective-permute-done.32 = bf16[256,512]{1,0:T(8,128)(2,1)S(1)} collective-permute-done((bf16[256,512]{1,0:T(8,128)(2,1)S(1)}, bf16[256,512]{1,0:T(8,128)(2,1)S(1)}, u32[]{:S(2)}, u32[]{:S(2)}) %collective-permute-start.32) | collective-permute-done | bytes 262176 | tf_op jit(solution)/shard_map/ppermute | solution.py:225
  (163 shorter events, 80.5 us)
Async XLA Ops:
  32.2 38.4 %collective-permute-start.22 = (bf16[512,1024]{1,0:T(8,128)(2,1)}, bf16[512,1024]{1,0:T(8,128)(2,1)}, u32[]{:S(2)}, u32[]{:S(2)}) collective-permute-start(bf16[512,1024]{1,0:T(8,128)(2,1)} %get-tuple-element.20.refs_0_.refs_8_), channel_id=1, source_target_pairs={{0,8},{8,0},{16,24},{24,16},{1,9},{9,1},{17,25},{25,17},{2,10},{10... | collective-permute-start | bytes 3145736 | tf_op jit(solution)/shard_map/ppermute | solution.py:219
  37.2 24.7 %collective-permute-start.6 = (bf16[1,128,1024]{2,1,0:T(8,128)(2,1)}, bf16[1,128,1024]{2,1,0:T(8,128)(2,1)S(1)}, u32[]{:S(2)}, u32[]{:S(2)}) collective-permute-start(bf16[1,128,1024]{2,1,0:T(8,128)(2,1)} %get-tuple-element.51), channel_id=1, source_target_pairs={{0,8},{8,0},{16,24},{24,16},{1,9},{9,1},{17,25},{25,17},{2,10},{10... | collective-permute-start | bytes 786440 | tf_op jit(solution)/shard_map/ppermute | solution.py:219
  37.7 36.3 %collective-permute-start.23 = (bf16[512,1024]{1,0:T(8,128)(2,1)}, bf16[512,1024]{1,0:T(8,128)(2,1)S(1)}, u32[]{:S(2)}, u32[]{:S(2)}) collective-permute-start(bf16[512,1024]{1,0:T(8,128)(2,1)} %get-tuple-element.20.refs_0_.refs_8_), channel_id=1, source_target_pairs={{0,16},{8,24},{16,0},{24,8},{1,17},{9,25},{17,1},{25,9},{2,18},{10... | collective-permute-start | bytes 3145736 | tf_op jit(solution)/shard_map/ppermute | solution.py:219
  38.3 28.6 %collective-permute-start.7 = (bf16[1,128,1024]{2,1,0:T(8,128)(2,1)}, bf16[1,128,1024]{2,1,0:T(8,128)(2,1)S(1)}, u32[]{:S(2)}, u32[]{:S(2)}) collective-permute-start(bf16[1,128,1024]{2,1,0:T(8,128)(2,1)} %get-tuple-element.49), channel_id=1, source_target_pairs={{0,16},{8,24},{16,0},{24,8},{1,17},{9,25},{17,1},{25,9},{2,18},{10... | collective-permute-start | bytes 786440 | tf_op jit(solution)/shard_map/ppermute | solution.py:219
  66.9 83.9 %collective-permute-start.8 = (bf16[2,512,1024]{2,1,0:T(8,128)(2,1)S(1)}, bf16[2,512,1024]{2,1,0:T(8,128)(2,1)S(1)}, u32[]{:S(2)}, u32[]{:S(2)}) collective-permute-start(bf16[2,512,1024]{2,1,0:T(8,128)(2,1)S(1)} %constant_dynamic-update-slice_fusion.mine_ref), channel_id=1, source_target_pairs={{0,1},{1,0},{2,3},{3,2},{4,5},{5,4},{6,7},{7,6},{8,9},{9,8},{10,11... | collective-permute-start | bytes 6291464 | tf_op jit(solution)/shard_map/ppermute | solution.py:222
  70.6 41.7 %collective-permute-start.14 = (bf16[64,5120]{1,0:T(8,128)(2,1)S(1)}, bf16[64,5120]{1,0:T(8,128)(2,1)S(1)}, u32[]{:S(2)}, u32[]{:S(2)}) collective-permute-start(bf16[64,5120]{1,0:T(8,128)(2,1)S(1)} %copy-done.3), channel_id=1, source_target_pairs={{0,2},{1,3},{2,4},{3,5},{4,6},{5,7},{6,0},{7,1},{8,10},{9,11},{10,... | collective-permute-start | bytes 1966088 | tf_op jit(solution)/shard_map/ppermute | solution.py:225
  74.1 76.1 %collective-permute-start.26 = (bf16[512,1024]{1,0:T(8,128)(2,1)}, bf16[512,1024]{1,0:T(8,128)(2,1)S(1)}, u32[]{:S(2)}, u32[]{:S(2)}) collective-permute-start(bf16[512,1024]{1,0:T(8,128)(2,1)} %get-tuple-element.23.refs_0_.refs_13_), channel_id=1, source_target_pairs={{0,8},{8,0},{16,24},{24,16},{1,9},{9,1},{17,25},{25,17},{2,10},{10... | collective-permute-start | bytes 3145736 | tf_op jit(solution)/shard_map/ppermute | solution.py:219
  82.5 30.6 %collective-permute-start.16 = (bf16[64,5120]{1,0:T(8,128)(2,1)S(1)}, bf16[64,5120]{1,0:T(8,128)(2,1)}, u32[]{:S(2)}, u32[]{:S(2)}) collective-permute-start(bf16[64,5120]{1,0:T(8,128)(2,1)S(1)} %copy-done.3), channel_id=1, source_target_pairs={{0,6},{1,7},{2,0},{3,1},{4,2},{5,3},{6,4},{7,5},{8,14},{9,15},{10,... | collective-permute-start | bytes 1966088 | tf_op jit(solution)/shard_map/ppermute | solution.py:225
  85.6 25.2 %collective-permute-start.11 = (bf16[256,512]{1,0:T(8,128)(2,1)S(1)}, bf16[256,512]{1,0:T(8,128)(2,1)S(1)}, u32[]{:S(2)}, u32[]{:S(2)}) collective-permute-start(bf16[256,512]{1,0:T(8,128)(2,1)S(1)} %slice.74), channel_id=1, source_target_pairs={{0,8},{8,0},{16,24},{24,16},{1,9},{9,1},{17,25},{25,17},{2,10},{10... | collective-permute-start | bytes 786440 | tf_op jit(solution)/shard_map/ppermute | solution.py:219
  110.8 39.8 %collective-permute-start.27 = (bf16[512,1024]{1,0:T(8,128)(2,1)}, bf16[512,1024]{1,0:T(8,128)(2,1)S(1)}, u32[]{:S(2)}, u32[]{:S(2)}) collective-permute-start(bf16[512,1024]{1,0:T(8,128)(2,1)} %get-tuple-element.23.refs_0_.refs_13_), channel_id=1, source_target_pairs={{0,16},{8,24},{16,0},{24,8},{1,17},{9,25},{17,1},{25,9},{2,18},{10... | collective-permute-start | bytes 3145736 | tf_op jit(solution)/shard_map/ppermute | solution.py:219
  112.4 28.3 %collective-permute-start.12 = (bf16[256,512]{1,0:T(8,128)(2,1)S(1)}, bf16[256,512]{1,0:T(8,128)(2,1)S(1)}, u32[]{:S(2)}, u32[]{:S(2)}) collective-permute-start(bf16[256,512]{1,0:T(8,128)(2,1)S(1)} %slice.75), channel_id=1, source_target_pairs={{0,16},{8,24},{16,0},{24,8},{1,17},{9,25},{17,1},{25,9},{2,18},{10... | collective-permute-start | bytes 786440 | tf_op jit(solution)/shard_map/ppermute | solution.py:219
  113.0 30.7 %collective-permute-start.18 = (bf16[32,5120]{1,0:T(8,128)(2,1)S(1)}, bf16[32,5120]{1,0:T(8,128)(2,1)}, u32[]{:S(2)}, u32[]{:S(2)}) collective-permute-start(bf16[32,5120]{1,0:T(8,128)(2,1)S(1)} %slice.76), channel_id=1, source_target_pairs={{0,2},{1,3},{2,4},{3,5},{4,6},{5,7},{6,0},{7,1},{8,10},{9,11},{10,... | collective-permute-start | bytes 983048 | tf_op jit(solution)/shard_map/ppermute | solution.py:225
  143.8 22.2 %collective-permute-start.13 = (bf16[64,5120]{1,0:T(8,128)(2,1)S(1)}, bf16[64,5120]{1,0:T(8,128)(2,1)}, u32[]{:S(2)}, u32[]{:S(2)}) collective-permute-start(bf16[64,5120]{1,0:T(8,128)(2,1)S(1)} %copy-done.3), channel_id=1, source_target_pairs={{0,1},{1,0},{2,3},{3,2},{4,5},{5,4},{6,7},{7,6},{8,9},{9,8},{10,11... | collective-permute-start | bytes 1966088 | tf_op jit(solution)/shard_map/ppermute | solution.py:222
  150.2 19.4 %collective-permute-start.15 = (bf16[64,5120]{1,0:T(8,128)(2,1)S(1)}, bf16[64,5120]{1,0:T(8,128)(2,1)}, u32[]{:S(2)}, u32[]{:S(2)}) collective-permute-start(bf16[64,5120]{1,0:T(8,128)(2,1)S(1)} %collective-permute-done.14.refs_2_), channel_id=1, source_target_pairs={{0,1},{1,0},{2,3},{3,2},{4,5},{5,4},{6,7},{7,6},{8,9},{9,8},{10,11... | collective-permute-start | bytes 1966088 | tf_op jit(solution)/shard_map/ppermute | solution.py:222
  150.2 20.0 %collective-permute-start.17 = (bf16[64,5120]{1,0:T(8,128)(2,1)}, bf16[64,5120]{1,0:T(8,128)(2,1)}, u32[]{:S(2)}, u32[]{:S(2)}) collective-permute-start(bf16[64,5120]{1,0:T(8,128)(2,1)} %collective-permute-done.16.refs_4_), channel_id=1, source_target_pairs={{0,1},{1,0},{2,3},{3,2},{4,5},{5,4},{6,7},{7,6},{8,9},{9,8},{10,11... | collective-permute-start | bytes 1966088 | tf_op jit(solution)/shard_map/ppermute | solution.py:222
  166.0 24.7 %collective-permute-start.24 = (bf16[256,1024]{1,0:T(8,128)(2,1)S(1)}, bf16[256,1024]{1,0:T(8,128)(2,1)S(1)}, u32[]{:S(2)}, u32[]{:S(2)}) collective-permute-start(bf16[256,1024]{1,0:T(8,128)(2,1)S(1)} %copy-done.6), channel_id=1, source_target_pairs={{0,8},{8,0},{16,24},{24,16},{1,9},{9,1},{17,25},{25,17},{2,10},{10... | collective-permute-start | bytes 1572872 | tf_op jit(solution)/shard_map/ppermute | solution.py:219
  167.6 23.2 %collective-permute-start.25 = (bf16[256,1024]{1,0:T(8,128)(2,1)S(1)}, bf16[256,1024]{1,0:T(8,128)(2,1)S(1)}, u32[]{:S(2)}, u32[]{:S(2)}) collective-permute-start(bf16[256,1024]{1,0:T(8,128)(2,1)S(1)} %copy-done.5), channel_id=1, source_target_pairs={{0,16},{8,24},{16,0},{24,8},{1,17},{9,25},{17,1},{25,9},{2,18},{10... | collective-permute-start | bytes 1572872 | tf_op jit(solution)/shard_map/ppermute | solution.py:219
  169.0 60.3 %collective-permute-start.28 = (bf16[256,1024]{1,0:T(8,128)(2,1)S(1)}, bf16[256,1024]{1,0:T(8,128)(2,1)}, u32[]{:S(2)}, u32[]{:S(2)}) collective-permute-start(bf16[256,1024]{1,0:T(8,128)(2,1)S(1)} %slice.80), channel_id=1, source_target_pairs={{0,8},{8,0},{16,24},{24,16},{1,9},{9,1},{17,25},{25,17},{2,10},{10... | collective-permute-start | bytes 1572872 | tf_op jit(solution)/shard_map/ppermute | solution.py:219
  169.6 59.7 %collective-permute-start.29 = (bf16[256,1024]{1,0:T(8,128)(2,1)S(1)}, bf16[256,1024]{1,0:T(8,128)(2,1)S(1)}, u32[]{:S(2)}, u32[]{:S(2)}) collective-permute-start(bf16[256,1024]{1,0:T(8,128)(2,1)S(1)} %slice.81), channel_id=1, source_target_pairs={{0,16},{8,24},{16,0},{24,8},{1,17},{9,25},{17,1},{25,9},{2,18},{10... | collective-permute-start | bytes 1572872 | tf_op jit(solution)/shard_map/ppermute | solution.py:219
  302.5 26.6 %collective-permute-start.32 = (bf16[256,512]{1,0:T(8,128)(2,1)S(1)}, bf16[256,512]{1,0:T(8,128)(2,1)S(1)}, u32[]{:S(2)}, u32[]{:S(2)}) collective-permute-start(bf16[256,512]{1,0:T(8,128)(2,1)S(1)} %get-tuple-element.45), channel_id=1, source_target_pairs={{0,4},{1,5},{2,6},{3,7},{4,0},{5,1},{6,2},{7,3},{8,12},{9,13},{10,... | collective-permute-start | bytes 786440 | tf_op jit(solution)/shard_map/ppermute | solution.py:225
  305.4 23.7 %collective-permute-start.31 = (bf16[256,512]{1,0:T(8,128)(2,1)S(1)}, bf16[256,512]{1,0:T(8,128)(2,1)S(1)}, u32[]{:S(2)}, u32[]{:S(2)}) collective-permute-start(bf16[256,512]{1,0:T(8,128)(2,1)S(1)} %get-tuple-element.43), channel_id=1, source_target_pairs={{0,2},{1,3},{2,4},{3,5},{4,6},{5,7},{6,0},{7,1},{8,10},{9,11},{10,... | collective-permute-start | bytes 786440 | tf_op jit(solution)/shard_map/ppermute | solution.py:225
  310.4 22.0 %collective-permute-start.43 = (bf16[256,128]{1,0:T(8,128)(2,1)S(1)}, bf16[256,128]{1,0:T(8,128)(2,1)S(1)}, u32[]{:S(2)}, u32[]{:S(2)}) collective-permute-start(bf16[256,128]{1,0:T(8,128)(2,1)S(1)} %get-tuple-element.57), channel_id=1, source_target_pairs={{0,6},{1,7},{2,0},{3,1},{4,2},{5,3},{6,4},{7,5},{8,14},{9,15},{10,... | collective-permute-start | bytes 196616 | tf_op jit(solution)/shard_map/ppermute | solution.py:225
  313.6 19.3 %collective-permute-start.42 = (bf16[256,128]{1,0:T(8,128)(2,1)S(1)}, bf16[256,128]{1,0:T(8,128)(2,1)S(1)}, u32[]{:S(2)}, u32[]{:S(2)}) collective-permute-start(bf16[256,128]{1,0:T(8,128)(2,1)S(1)} %get-tuple-element.58), channel_id=1, source_target_pairs={{0,4},{1,5},{2,6},{3,7},{4,0},{5,1},{6,2},{7,3},{8,12},{9,13},{10,... | collective-permute-start | bytes 196616 | tf_op jit(solution)/shard_map/ppermute | solution.py:225
  313.6 19.3 %collective-permute-start.41 = (bf16[256,128]{1,0:T(8,128)(2,1)S(1)}, bf16[256,128]{1,0:T(8,128)(2,1)S(1)}, u32[]{:S(2)}, u32[]{:S(2)}) collective-permute-start(bf16[256,128]{1,0:T(8,128)(2,1)S(1)} %get-tuple-element.56), channel_id=1, source_target_pairs={{0,2},{1,3},{2,4},{3,5},{4,6},{5,7},{6,0},{7,1},{8,10},{9,11},{10,... | collective-permute-start | bytes 196616 | tf_op jit(solution)/shard_map/ppermute | solution.py:225
  (44 other events, 650.8 us)
